TPU v7x, 32 devices: a whole 2x2x4 slice. The times are simulated.
32 devices in a mesh: dp: 16 (over z, y, x), mp: 2 (over core).
Axes of the slice: x: 2, y: 2, z: 4, core: 2. Of those that a mesh axis runs over, the one named last changes fastest.
Arguments:
- clean: float32 [64, 3, 4096], P(('dp', 'mp')), may hold values from -1 to 1
- noise: float32 [64, 3, 4096], P(('dp', 'mp')), may hold values from -12 to 12
- lowres: float32 [64, 3, 4096], P(('dp', 'mp')), may hold values from -1 to 1
- aug_noise: float32 [64, 3, 4096], P(('dp', 'mp')), may hold values from -5 to 5
- timesteps: int32 [64], P(('dp', 'mp')), may hold values from 0 to 999
- aug_levels: int32 [64], P(('dp', 'mp')), may hold values from 0 to 999
- lengths: int32 [64], P(('dp', 'mp')), may hold values from 1 to 128
- text: bfloat16 [64, 128, 4096], P(('dp', 'mp')), may hold values from -160 to 160
- w_stem: float32 [6, 128], replicated, may hold values from -2.5 to 2.5
- w_time: float32 [256, 256], replicated, may hold values from -0.375 to 0.375
- conv_one: bfloat16 [1152, 128], replicated, may hold values from -0.1875 to 0.1875
- conv_two: bfloat16 [1152, 128], replicated, may hold values from -0.1875 to 0.1875
- kv_weight: bfloat16 [4096, 256], P('mp'), may hold values from -0.09375 to 0.09375
- w_query: bfloat16 [128, 128], replicated, may hold values from -0.5 to 0.5
- w_output: bfloat16 [128, 128], replicated, may hold values from -0.5 to 0.5
- w_head: bfloat16 [3, 128], replicated, may hold values from -0.5 to 0.5
Outputs:
- conv_one_update: float32 [1152, 128], P(('dp', 'mp'))
- conv_two_update: float32 [1152, 128], P(('dp', 'mp'))
- kv_update: float32 [4096, 256], P('mp', 'dp')
- loss_mean: float32 [], replicated
All inputs are finite; a program needn't handle non-finite values.
Results may differ from a plain program's by a relative error of at most 0.03.
The roundings to bfloat16 on the way count: a program that leaves them out, or rounds other values in their place, can miss the bound.
Values may be sent and summed in bfloat16 or wider, within the bound.
No kernel may reach another device: no remote copies, remote signals or barrier semaphores. Data moves between devices by JAX's collectives and lax.ppermute only.
A program may use at most 128 MiB of HBM per device.

v0:
```python
import math
import jax
import jax.numpy as jnp
from jax import lax
from jax.sharding import PartitionSpec as P

S = 64
GROUPS = 32
HEADS = 2
HEAD_DIM = 64
FREQS = 64
STEPS = 1000


def signal_level(index):
    ratio = (index.astype(jnp.float32) / STEPS + 0.008) / 1.008
    cosine = jnp.cos(ratio * (math.pi / 2.0))
    return cosine * cosine


def sinusoid(index):
    freqs = jnp.exp(-math.log(10000.0) * jnp.arange(FREQS, dtype=jnp.float32) / FREQS)
    angles = index.astype(jnp.float32) * freqs
    return jnp.concatenate([jnp.sin(angles), jnp.cos(angles)])


def prepare(clean, noise, lowres, aug_noise, tstep, level, w_stem, w_time):
    signal = signal_level(tstep)
    aug_signal = signal_level(level)
    noisy = jnp.sqrt(signal) * clean + jnp.sqrt(1.0 - signal) * noise
    low_noisy = jnp.sqrt(aug_signal) * lowres + jnp.sqrt(1.0 - aug_signal) * aug_noise
    stacked = jnp.concatenate([noisy, low_noisy], axis=0)
    h_start = jnp.einsum("kp,kc->pc", stacked, w_stem, precision=lax.Precision.HIGHEST)
    feature = jnp.concatenate([sinusoid(tstep), sinusoid(level)])[None, :]
    embed = jax.nn.silu(jnp.dot(feature, w_time, precision=lax.Precision.HIGHEST))[0]
    channels = w_stem.shape[1]
    return (h_start, embed[:channels], embed[channels:])


def group_matrix(channels):
    members = channels // GROUPS
    labels = jnp.arange(channels) // members
    return (labels[:, None] == labels[None, :]).astype(jnp.float32) / members


def group_norm(values, grouping):
    average = jnp.dot(
        jnp.mean(values, axis=0, keepdims=True), grouping, precision=lax.Precision.HIGHEST
    )
    centred = values - average
    spread = jnp.dot(
        jnp.mean(centred * centred, axis=0, keepdims=True),
        grouping,
        precision=lax.Precision.HIGHEST,
    )
    return centred * lax.rsqrt(spread + 1e-05)


def convolve(activation, weight):
    channels = weight.shape[1]
    kernel = weight.reshape(3, 3, channels, channels)
    picture = activation.reshape(1, S, S, channels)
    result = lax.conv_general_dilated(
        picture,
        kernel,
        (1, 1),
        "SAME",
        dimension_numbers=("NHWC", "HWIO", "NHWC"),
        preferred_element_type=jnp.float32,
    )
    return result.reshape(S * S, channels)


def image_loss(
    conv_one, conv_two, keys_values, h_start, scale, shift, keep, w_query, w_output, w_head, noise
):
    channels = conv_one.shape[1]
    grouping = group_matrix(channels)
    act_one = jax.nn.silu(group_norm(h_start, grouping)).astype(jnp.bfloat16)
    conv_out_one = convolve(act_one, conv_one)
    act_two = jax.nn.silu(group_norm(conv_out_one, grouping) * (1.0 + scale) + shift).astype(
        jnp.bfloat16
    )
    h_mid = h_start + convolve(act_two, conv_two)
    normed = group_norm(h_mid, grouping).astype(jnp.bfloat16)
    queries = (
        jnp.dot(normed, w_query, preferred_element_type=jnp.float32) * HEAD_DIM ** (-0.5)
    ).astype(jnp.bfloat16)
    width = w_query.shape[1]
    pieces = []
    for head_index in range(HEADS):
        lower = head_index * HEAD_DIM
        upper = lower + HEAD_DIM
        scores = jnp.dot(
            queries[:, lower:upper],
            keys_values[:, lower:upper].T,
            preferred_element_type=jnp.float32,
        )
        scores = jnp.where(keep[None, :], scores, -1e30)
        highest = jnp.max(scores, axis=1, keepdims=True)
        weights = jnp.exp(scores - highest)
        probs = (weights / jnp.sum(weights, axis=1, keepdims=True)).astype(jnp.bfloat16)
        pieces.append(
            jnp.dot(
                probs,
                keys_values[:, width + lower : width + upper],
                preferred_element_type=jnp.float32,
            )
        )
    attended = jnp.concatenate(pieces, axis=1).astype(jnp.bfloat16)
    h_out = h_mid + jnp.dot(attended, w_output, preferred_element_type=jnp.float32)
    pred = jnp.einsum(
        "kc,pc->kp", w_head, h_out.astype(jnp.bfloat16), preferred_element_type=jnp.float32
    )
    error = pred - noise
    return jnp.sum(error * error)


def local(
    clean,
    noise,
    lowres,
    aug_noise,
    timesteps,
    aug_levels,
    lengths,
    text,
    w_stem,
    w_time,
    conv_one,
    conv_two,
    kv_weight,
    w_query,
    w_output,
    w_head,
):
    images = clean.shape[0]
    tokens = text.shape[1]
    features = text.shape[2]
    width = kv_weight.shape[1]
    half = kv_weight.shape[0]
    piece = lax.all_gather(kv_weight, "mp", axis=0, tiled=True)
    flat = jnp.dot(
        text.reshape(images * tokens, piece.shape[0]), piece, preferred_element_type=jnp.float32
    )
    summed = flat.reshape(images, tokens, width)
    keys_values = summed.astype(jnp.bfloat16)

    def one_image(items):
        clean_i, noise_i, low_i, aug_i, tstep, level, length, pairs = items
        h_start, scale, shift = prepare(
            clean_i, noise_i, low_i, aug_i, tstep, level, w_stem, w_time
        )
        keep = jnp.arange(tokens) < length
        value, pullback = jax.vjp(
            lambda first, second, third: image_loss(
                first,
                second,
                third,
                h_start,
                scale,
                shift,
                keep,
                w_query,
                w_output,
                w_head,
                noise_i,
            ),
            conv_one,
            conv_two,
            pairs,
        )
        part_one, part_two, part_kv = pullback(jnp.ones((), jnp.float32))
        return (part_one, part_two, part_kv, value)

    parts_one, parts_two, parts_kv, values = lax.map(
        one_image, (clean, noise, lowres, aug_noise, timesteps, aug_levels, lengths, keys_values)
    )
    local_one = jnp.sum(parts_one.astype(jnp.float32), axis=0)
    local_two = jnp.sum(parts_two.astype(jnp.float32), axis=0)
    local_loss = jnp.sum(values)
    loss_total = lax.psum(local_loss, ("dp", "mp"))
    grad_one, grad_two = (
        lax.psum_scatter(local_one, ("dp", "mp"), scatter_dimension=0, tiled=True),
        lax.psum_scatter(local_two, ("dp", "mp"), scatter_dimension=0, tiled=True),
    )
    full_grad = lax.dot_general(
        text.reshape(-1, features),
        parts_kv.reshape(-1, width),
        (((0,), (0,)), ((), ())),
        preferred_element_type=jnp.float32,
    )
    row_share = lax.psum_scatter(full_grad, "mp", scatter_dimension=0, tiled=True)
    grad_kv = lax.psum_scatter(row_share, "dp", scatter_dimension=1, tiled=True)
    square_one = jnp.sum(grad_one * grad_one)
    square_two = jnp.sum(grad_two * grad_two)
    square_kv = jnp.sum(grad_kv * grad_kv)
    total_one, total_two, total_kv = lax.psum((square_one, square_two, square_kv), ("dp", "mp"))
    conv_count = conv_one.shape[0] * conv_one.shape[1]
    kv_count = half * lax.axis_size("mp") * width
    conv_one_update = grad_one * lax.rsqrt(total_one / conv_count + 1e-06)
    conv_two_update = grad_two * lax.rsqrt(total_two / conv_count + 1e-06)
    kv_update = grad_kv * lax.rsqrt(total_kv / kv_count + 1e-06)
    loss_mean = loss_total / (
        images * lax.axis_size(("dp", "mp")) * clean.shape[1] * clean.shape[2]
    )
    return (conv_one_update, conv_two_update, kv_update, loss_mean)


def solution(mesh):
    return jax.shard_map(
        local,
        mesh=mesh,
        in_specs=(
            P(("dp", "mp"), None, None),
            P(("dp", "mp"), None, None),
            P(("dp", "mp"), None, None),
            P(("dp", "mp"), None, None),
            P(("dp", "mp")),
            P(("dp", "mp")),
            P(("dp", "mp")),
            P(("dp", "mp"), None, None),
            P(),
            P(),
            P(),
            P(),
            P("mp", None),
            P(),
            P(),
            P(),
        ),
        out_specs=(P(("dp", "mp"), None), P(("dp", "mp"), None), P("mp", "dp"), P()),
        check_vma=False,
    )
```

profile of v0, /device:TPU:0, one launch (start us, length us, event | category | flops | bytes accessed | tf_op | source)
XLA Modules:
  0.0 415.6 jit_solution(3835564456848357906)
XLA Ops:
  8.1 14.8 %all-gather.2.cloned.1.call-done = bf16[4096,256]{1,0:T(8,128)(2,1)} async-done(((bf16[2048,256]{1,0:T(8,128)(2,1)}), bf16[4096,256]{1,0:T(8,128)(2,1)}) %all-gather.2.cloned.1.call-update) | async-done | bytes 2097168 | tf_op jit(solution)/shard_map/all_gather | solution.py:142
  25.8 184.8 %while.19 = (s32[]{:T(128)}, bf16[2,1152,128]{2,1,0:T(8,128)(2,1)}, bf16[2,1152,128]{2,1,0:T(8,128)(2,1)}, bf16[2,128,256]{1,2,0:T(8,128)(2,1)}, f32[2]{0:T(128)...) while((s32[]{:T(128)}, bf16[2,1152,128]{2,1,0:T(8,128)(2,1)}, ...), condition=%wide.region_22.23_spmd, body=%wide.region_0.22_spmd.sunk | while | flops 8245876736 | bytes 325935616 | solution.py:176
  33.1 3.5 fusion.464
  40.1 3.0 select_reduce_fusion.8
  48.2 3.1 fusion.476
  66.6 3.9 multiply_reduce_fusion.17
  88.3 5.1 %select_reduce_fusion.10 = (f32[128]{0:T(128)S(1)}, f32[64,8,9,128]{3,1,2,0:T(8,128)S(1)}) fusion(f32[64,8,9,128]{3,1,2,0:T(8,128)S(1)} %copy-done.8, f32[128]{0:T(128)S(1)} %copy-done.40, pred[8,9]{0,1:T(8,128)(4,1)} %get-tuple-element.839, f32[128]{0:T(128)S(1)} %copy-done.48, f32[128]{0:T(128)S(1)} %copy-done.46, f32[128]{0:T(128)S(1)} %copy-done.50, ...), kind=kOutput, calls=%fused_computation.51.clone.1 | convolution fusion | flops 1360920448 | bytes 6425160 | tf_op jit(solution)/shard_map/while/body/eval_jaxpr/transpose(jvp())/conv_general_dilated | solution.py:63
  98.4 5.0 %fusion.499 = bf16[3,3,128,128,1]{3,2,1,4,0:T(8,128)(2,1)S(1)} fusion(bf16[64,8,9,128,1]{3,1,4,2,0:T(8,128)(2,1)S(1)} %fusion.495, bf16[64,8,9,128,1]{3,1,4,2,0:T(8,128)(2,1)S(1)} %copy.137, bf16[64,8,9,128,1]{3,1,4,2,0:T(8,128)(2,1)S(1)} %fusion.496, f32[128]{0:T(128)S(1)} %fusion.498, pred[8,9]{0,1:T(8,128)(4,1)} %get-tuple-element.839, ...), kind=kOutput, calls=%fused_computation.101.clone.1 | convolution fusion | flops 1360281600 | bytes 8554568 | tf_op jit(solution)/shard_map/while/body/eval_jaxpr/transpose(jvp())/conv_general_dilated | solution.py:63
  106.5 4.8 %fusion.492 = bf16[3,3,128,128,1]{3,2,1,4,0:T(8,128)(2,1)S(1)} fusion(bf16[64,8,9,128,1]{3,0,2,1,4:T(8,128)(2,1)S(1)} %bitcast.331, bf16[64,8,9,128,1]{3,1,2,0,4:T(8,128)(2,1)S(1)} %maximum_bitcast_fusion.8, bf16[64,8,9,128,1]{3,1,2,0,4:T(8,128)(2,1)S(1)} %fusion.491, bf16[64,8,9,128,1]{3,1,2,0,4:T(8,128)(2,1)S(1)} %maximum_bitcast_fusion.9), kind=kOutput, calls=%fused_computation.100.clone.1 | convolution fusion | flops 1348337664 | bytes 5013504 | tf_op jit(solution)/shard_map/while/body/eval_jaxpr/transpose(jvp())/conv_general_dilated | solution.py:63
  123.4 3.5 fusion.464
  130.5 3.0 select_reduce_fusion.8
  138.7 3.1 fusion.476
  157.2 3.9 multiply_reduce_fusion.17
  178.9 4.9 %select_reduce_fusion.10 = (f32[128]{0:T(128)S(1)}, f32[64,8,9,128]{3,1,2,0:T(8,128)S(1)}) fusion(f32[64,8,9,128]{3,1,2,0:T(8,128)S(1)} %copy-done.8, f32[128]{0:T(128)S(1)} %copy-done.40, pred[8,9]{0,1:T(8,128)(4,1)} %get-tuple-element.839, f32[128]{0:T(128)S(1)} %copy-done.48, f32[128]{0:T(128)S(1)} %copy-done.46, f32[128]{0:T(128)S(1)} %copy-done.50, ...), kind=kOutput, calls=%fused_computation.51.clone.1 | convolution fusion | flops 1360920448 | bytes 6425160 | tf_op jit(solution)/shard_map/while/body/eval_jaxpr/transpose(jvp())/conv_general_dilated | solution.py:63
  188.8 5.0 %fusion.499 = bf16[3,3,128,128,1]{3,2,1,4,0:T(8,128)(2,1)S(1)} fusion(bf16[64,8,9,128,1]{3,1,4,2,0:T(8,128)(2,1)S(1)} %fusion.495, bf16[64,8,9,128,1]{3,1,4,2,0:T(8,128)(2,1)S(1)} %copy.137, bf16[64,8,9,128,1]{3,1,4,2,0:T(8,128)(2,1)S(1)} %fusion.496, f32[128]{0:T(128)S(1)} %fusion.498, pred[8,9]{0,1:T(8,128)(4,1)} %get-tuple-element.839, ...), kind=kOutput, calls=%fused_computation.101.clone.1 | convolution fusion | flops 1360281600 | bytes 8554568 | tf_op jit(solution)/shard_map/while/body/eval_jaxpr/transpose(jvp())/conv_general_dilated | solution.py:63
  196.8 5.0 %fusion.492 = bf16[3,3,128,128,1]{3,2,1,4,0:T(8,128)(2,1)S(1)} fusion(bf16[64,8,9,128,1]{3,0,2,1,4:T(8,128)(2,1)S(1)} %bitcast.331, bf16[64,8,9,128,1]{3,1,2,0,4:T(8,128)(2,1)S(1)} %maximum_bitcast_fusion.8, bf16[64,8,9,128,1]{3,1,2,0,4:T(8,128)(2,1)S(1)} %fusion.491, bf16[64,8,9,128,1]{3,1,2,0,4:T(8,128)(2,1)S(1)} %maximum_bitcast_fusion.9), kind=kOutput, calls=%fused_computation.100.clone.1 | convolution fusion | flops 1348337664 | bytes 5013504 | tf_op jit(solution)/shard_map/while/body/eval_jaxpr/transpose(jvp())/conv_general_dilated | solution.py:63
  210.7 3.6 convolution_bitcast_fusion.11
  214.4 13.2 %reduce-scatter.7.cloned.1.call-done = f32[2048,256]{0,1:T(8,128)} async-done(((f32[4096,256]{0,1:T(8,128)}), f32[2048,256]{0,1:T(8,128)}) %reduce-scatter.7.cloned.1.call-update) | async-done | bytes 2097168 | tf_op jit(solution)/shard_map/reduce_scatter | solution.py:193
  229.2 86.5 %fusion.288 = (f32[48,128]{1,0:T(8,128)S(1)}, f32[48,128]{1,0:T(8,128)S(1)}) fusion(f32[1152,128]{1,0:T(8,128)S(1)} %get-tuple-element.470, f32[1152,128]{1,0:T(8,128)S(1)} %get-tuple-element.469), kind=kCustom, calls=%all-reduce-scatter.2 | all-reduce-scatter fusion | flops 393217 | bytes 1228800
  322.2 7.0 %collective-permute-start.7 = (f32[36,128]{1,0:T(8,128)S(1)}, f32[36,128]{1,0:T(8,128)S(1)}, u32[]{:S(2)}, u32[]{:S(2)}) collective-permute-start(f32[36,128]{1,0:T(8,128)S(1)} %slice.90), channel_id=1, source_target_pairs={{0,8},{1,9},{2,10},{3,11},{4,12},{5,13},{6,14},{7,15},{8,16},{9,17... | collective-permute-start | bytes 55304
  332.0 4.9 %collective-permute-start.8 = (f32[48,128]{1,0:T(8,128)S(1)}, f32[48,128]{1,0:T(8,128)S(1)}, u32[]{:S(2)}, u32[]{:S(2)}) collective-permute-start(f32[48,128]{1,0:T(8,128)S(1)} %get-tuple-element.418), channel_id=1, source_target_pairs={{0,1},{1,2},{2,3},{3,4},{4,5},{5,6},{6,7},{7,8},{8,9},{9,10},{10,1... | collective-permute-start | bytes 73736
  342.3 3.2 collective-permute-start.1
  352.9 3.0 collective-permute-start.5
  363.5 38.8 %all-reduce.10 = (f32[]{:T(128)}, f32[]{:T(128)}, f32[]{:T(128)}, f32[]{:T(128)}) all-reduce(f32[]{:T(128)} %multiply_reduce_fusion.8, f32[]{:T(128)} %multiply_reduce_fusion.7, f32[]{:T(128)} %multiply_reduce_fusion.6, f32[]{:T(128)} %reduce_sum.338), channel_id=1, replica_groups=mesh['dp'=16,'mp'=2] {'dp','mp'}, use_global_device_ids=true, to_apply=%region_26.27 | all-reduce | flops 4 | bytes 32 | tf_op jit(solution)/shard_map/psum | solution.py:198
  (514 shorter events, 148.5 us)
Async XLA Ops:
  7.2 15.7 %all-gather.2.cloned.1.call-start = ((), (), s32[]{:S(2)}) async-start(), calls=%async_computation.2 | async-start | bytes 3145728 | tf_op jit(solution)/shard_map/all_gather | solution.py:142
  7.9 219.7 %reduce-scatter.7.cloned.1.call-start = ((), (), s32[]{:S(2)}) async-start(), calls=%async_computation.3 | async-start | bytes 6291456 | tf_op jit(solution)/shard_map/reduce_scatter | solution.py:193
  8.0 17.8 %copy-start.26 = (bf16[128,128]{1,0:T(8,128)(2,1)S(1)}, bf16[128,128]{1,0:T(8,128)(2,1)}, u32[]{:S(2)}) copy-start(bf16[128,128]{1,0:T(8,128)(2,1)} %param.31) | copy-start | bytes 98308
  8.0 17.8 %copy-start.30 = (pred[8,9]{0,1:T(8,128)(4,1)S(1)}, pred[8,9]{0,1:T(8,128)(4,1)}, u32[]{:S(2)}) copy-start(pred[8,9]{0,1:T(8,128)(4,1)} %constant.595) | copy-start | bytes 220
  36.5 18.0 %copy-start.67 = (s32[128]{0:T(128)}, s32[128]{0:T(128)S(1)}, u32[]{:S(2)}) copy-start(s32[128]{0:T(128)S(1)} %and_select_fusion.2) | copy-start | bytes 1540 | tf_op jit(solution)/shard_map/while
  126.9 18.2 %copy-start.67 = (s32[128]{0:T(128)}, s32[128]{0:T(128)S(1)}, u32[]{:S(2)}) copy-start(s32[128]{0:T(128)S(1)} %and_select_fusion.2) | copy-start | bytes 1540 | tf_op jit(solution)/shard_map/while
  214.3 147.6 %reduce-scatter.9.cloned.1.call-start = ((), (), s32[]{:S(2)}) async-start(), calls=%async_computation.4 | async-start | bytes 2228224 | tf_op jit(solution)/shard_map/reduce_scatter | solution.py:194
  227.6 130.0 %copy-start.66 = (f32[2]{0:T(128)S(1)}, f32[2]{0:T(128)}, u32[]{:S(2)}) copy-start(f32[2]{0:T(128)} %get-tuple-element.971) | copy-start | bytes 28
  315.7 6.5 %collective-permute-start.15 = (f32[36,128]{1,0:T(8,128)S(1)}, f32[36,128]{1,0:T(8,128)S(1)}, u32[]{:S(2)}, u32[]{:S(2)}) collective-permute-start(f32[36,128]{1,0:T(8,128)S(1)} %slice.91), channel_id=1, source_target_pairs={{0,8},{1,9},{2,10},{3,11},{4,12},{5,13},{6,14},{7,15},{8,16},{9,17... | collective-permute-start | bytes 55304
  317.0 15.0 %collective-permute-start.10 = (f32[48,128]{1,0:T(8,128)S(1)}, f32[48,128]{1,0:T(8,128)S(1)}, u32[]{:S(2)}, u32[]{:S(2)}) collective-permute-start(f32[48,128]{1,0:T(8,128)S(1)} %get-tuple-element.418), channel_id=1, source_target_pairs={{0,3},{1,4},{2,5},{3,6},{4,7},{5,8},{6,9},{7,10},{8,11},{9,12},{10... | collective-permute-start | bytes 73736
  318.3 18.7 %collective-permute-start.11 = (f32[48,128]{1,0:T(8,128)S(1)}, f32[48,128]{1,0:T(8,128)S(1)}, u32[]{:S(2)}, u32[]{:S(2)}) collective-permute-start(f32[48,128]{1,0:T(8,128)S(1)} %get-tuple-element.418), channel_id=1, source_target_pairs={{0,4},{1,5},{2,6},{3,7},{4,8},{5,9},{6,10},{7,11},{8,12},{9,13},{1... | collective-permute-start | bytes 73736
  319.6 20.1 %collective-permute-start.12 = (f32[48,128]{1,0:T(8,128)S(1)}, f32[48,128]{1,0:T(8,128)S(1)}, u32[]{:S(2)}, u32[]{:S(2)}) collective-permute-start(f32[48,128]{1,0:T(8,128)S(1)} %get-tuple-element.418), channel_id=1, source_target_pairs={{0,5},{1,6},{2,7},{3,8},{4,9},{5,10},{6,11},{7,12},{8,13},{9,14},{... | collective-permute-start | bytes 73736
  320.9 21.4 %collective-permute-start.13 = (f32[48,128]{1,0:T(8,128)S(1)}, f32[48,128]{1,0:T(8,128)S(1)}, u32[]{:S(2)}, u32[]{:S(2)}) collective-permute-start(f32[48,128]{1,0:T(8,128)S(1)} %get-tuple-element.418), channel_id=1, source_target_pairs={{0,6},{1,7},{2,8},{3,9},{4,10},{5,11},{6,12},{7,13},{8,14},{9,15},... | collective-permute-start | bytes 73736
  322.2 8.5 %collective-permute-start.7 = (f32[36,128]{1,0:T(8,128)S(1)}, f32[36,128]{1,0:T(8,128)S(1)}, u32[]{:S(2)}, u32[]{:S(2)}) collective-permute-start(f32[36,128]{1,0:T(8,128)S(1)} %slice.90), channel_id=1, source_target_pairs={{0,8},{1,9},{2,10},{3,11},{4,12},{5,13},{6,14},{7,15},{8,16},{9,17... | collective-permute-start | bytes 55304
  330.7 14.8 %collective-permute-start.14 = (f32[48,128]{1,0:T(8,128)S(1)}, f32[48,128]{1,0:T(8,128)S(1)}, u32[]{:S(2)}, u32[]{:S(2)}) collective-permute-start(f32[48,128]{1,0:T(8,128)S(1)} %get-tuple-element.418), channel_id=1, source_target_pairs={{0,7},{1,8},{2,9},{3,10},{4,11},{5,12},{6,13},{7,14},{8,15},{9,16}... | collective-permute-start | bytes 73736
  332.0 16.5 %collective-permute-start.8 = (f32[48,128]{1,0:T(8,128)S(1)}, f32[48,128]{1,0:T(8,128)S(1)}, u32[]{:S(2)}, u32[]{:S(2)}) collective-permute-start(f32[48,128]{1,0:T(8,128)S(1)} %get-tuple-element.418), channel_id=1, source_target_pairs={{0,1},{1,2},{2,3},{3,4},{4,5},{5,6},{6,7},{7,8},{8,9},{9,10},{10,1... | collective-permute-start | bytes 73736
  336.9 14.0 %collective-permute-start.9 = (f32[48,128]{1,0:T(8,128)S(1)}, f32[48,128]{1,0:T(8,128)S(1)}, u32[]{:S(2)}, u32[]{:S(2)}) collective-permute-start(f32[48,128]{1,0:T(8,128)S(1)} %get-tuple-element.418), channel_id=1, source_target_pairs={{0,2},{1,3},{2,4},{3,5},{4,6},{5,7},{6,8},{7,9},{8,10},{9,11},{10,... | collective-permute-start | bytes 73736
  339.7 13.2 %collective-permute-start = (f32[48,128]{1,0:T(8,128)S(1)}, f32[48,128]{1,0:T(8,128)S(1)}, u32[]{:S(2)}, u32[]{:S(2)}) collective-permute-start(f32[48,128]{1,0:T(8,128)S(1)} %get-tuple-element.417), channel_id=1, source_target_pairs={{0,1},{1,2},{2,3},{3,4},{4,5},{5,6},{6,7},{7,8},{8,9},{9,10},{10,1... | collective-permute-start | bytes 73736
  342.3 13.6 %collective-permute-start.1 = (f32[48,128]{1,0:T(8,128)S(1)}, f32[48,128]{1,0:T(8,128)S(1)}, u32[]{:S(2)}, u32[]{:S(2)}) collective-permute-start(f32[48,128]{1,0:T(8,128)S(1)} %get-tuple-element.417), channel_id=1, source_target_pairs={{0,2},{1,3},{2,4},{3,5},{4,6},{5,7},{6,8},{7,9},{8,10},{9,11},{10,... | collective-permute-start | bytes 73736
  345.5 13.9 %collective-permute-start.2 = (f32[48,128]{1,0:T(8,128)S(1)}, f32[48,128]{1,0:T(8,128)S(1)}, u32[]{:S(2)}, u32[]{:S(2)}) collective-permute-start(f32[48,128]{1,0:T(8,128)S(1)} %get-tuple-element.417), channel_id=1, source_target_pairs={{0,3},{1,4},{2,5},{3,6},{4,7},{5,8},{6,9},{7,10},{8,11},{9,12},{10... | collective-permute-start | bytes 73736
  348.5 10.9 %collective-permute-start.3 = (f32[48,128]{1,0:T(8,128)S(1)}, f32[48,128]{1,0:T(8,128)S(1)}, u32[]{:S(2)}, u32[]{:S(2)}) collective-permute-start(f32[48,128]{1,0:T(8,128)S(1)} %get-tuple-element.417), channel_id=1, source_target_pairs={{0,4},{1,5},{2,6},{3,7},{4,8},{5,9},{6,10},{7,11},{8,12},{9,13},{1... | collective-permute-start | bytes 73736
  350.9 8.5 %collective-permute-start.4 = (f32[48,128]{1,0:T(8,128)S(1)}, f32[48,128]{1,0:T(8,128)S(1)}, u32[]{:S(2)}, u32[]{:S(2)}) collective-permute-start(f32[48,128]{1,0:T(8,128)S(1)} %get-tuple-element.417), channel_id=1, source_target_pairs={{0,5},{1,6},{2,7},{3,8},{4,9},{5,10},{6,11},{7,12},{8,13},{9,14},{... | collective-permute-start | bytes 73736
  352.9 6.5 %collective-permute-start.5 = (f32[48,128]{1,0:T(8,128)S(1)}, f32[48,128]{1,0:T(8,128)S(1)}, u32[]{:S(2)}, u32[]{:S(2)}) collective-permute-start(f32[48,128]{1,0:T(8,128)S(1)} %get-tuple-element.417), channel_id=1, source_target_pairs={{0,6},{1,7},{2,8},{3,9},{4,10},{5,11},{6,12},{7,13},{8,14},{9,15},... | collective-permute-start | bytes 73736
  355.9 3.5 collective-permute-start.6
  (129 other events, 388.2 us)
Sparse Core Ops, SparseCore 0:
  9.5 13.2 all-gather.1
  214.4 13.0 reduce-scatter.6
  229.9 82.9 reduce-scatter.8
where the time goes:
time: 419 us; the launch traced here: 416 us
  blocking collectives  125 us (30%)
  matrix products  95.9 us (23%)
  local copies, waits for them, and re-layouts  48.1 us (11%)
  other arithmetic  40.4 us (10%)
  starting transfers between devices  40.3 us (10%)
  waiting for transfers between devices  30.2 us (7%)
  between operations  18.3 us (4%)
  loops' own time  17.2 us (4%)
    unnamed x1, blocking collectives  86.5 us
    conv_general_dilated x10, matrix products, convolve(): lax.conv_general_dilated(picture, kernel, (1, 1), 'SAME', dimension_numbe...  41.9 us
    unnamed x16, starting transfers between devices  40.2 us
    psum x1, blocking collectives, local(): lax.psum((square_one, square_two, square_kv), ('dp', 'mp'))  38.8 us
    while x260, local copies, waits for them, and re-layouts  17.9 us
    another operation x1, loops' own time, local(): lax.map(one_image, (clean, noise, lowres, aug_noise, timesteps, aug_level...  17.2 us
    all_gather x1, waiting for transfers between devices, local(): piece = lax.all_gather(kv_weight, 'mp', axis=0, tiled=True)  14.8 us
    reduce_scatter x1, waiting for transfers between devices, local(): lax.psum_scatter(full_grad, 'mp', scatter_dimension=0, tiled=True)  13.2 us
  transfers between devices with their start and end apart: 19, of which 3 were waited for; matrix products, arithmetic and copies ran while one was open for 22% of the time, Pallas kernels for 0%

commit v1 on v0

--- a/solution.py
+++ b/solution.py
@@ -195,7 +195,9 @@
     square_one = jnp.sum(grad_one * grad_one)
     square_two = jnp.sum(grad_two * grad_two)
     square_kv = jnp.sum(grad_kv * grad_kv)
-    total_one, total_two, total_kv = lax.psum((square_one, square_two, square_kv), ("dp", "mp"))
+    total_one, total_two, total_kv = lax.psum(
+        lax.psum((square_one, square_two, square_kv), axis_name="mp"), "dp"
+    )
     conv_count = conv_one.shape[0] * conv_one.shape[1]
     kv_count = half * lax.axis_size("mp") * width
     conv_one_update = grad_one * lax.rsqrt(total_one / conv_count + 1e-06)

time: 419 us -> 463 us (1.11)
  blocking collectives: 125 us -> 169 us
    psum x1 -> x3, blocking collectives: 38.8 us -> 81.4 us  [the longest x1 41.1 us: local(): lax.psum(lax.psum((square_one, square_two, square_kv), axis_name='mp'), '...]
  transfers between devices with their start and end apart: 19 -> 19, of which waited for: 3 -> 3; matrix products, arithmetic and copies ran while one was open for 22% -> 20% of each run, Pallas kernels for 0% -> 0%
where the time goes in v1:
time: 463 us; the launch traced here: 460 us
  blocking collectives  169 us (37%)
  matrix products  95.9 us (21%)
  local copies, waits for them, and re-layouts  48.2 us (10%)
  other arithmetic  40.4 us (9%)
  starting transfers between devices  40.3 us (9%)
  waiting for transfers between devices  30.2 us (7%)
  between operations  18.2 us (4%)
  loops' own time  17.2 us (4%)
    unnamed x1, blocking collectives  87.8 us
    conv_general_dilated x10, matrix products, convolve(): lax.conv_general_dilated(picture, kernel, (1, 1), 'SAME', dimension_numbe...  41.9 us
    psum x1, blocking collectives, local(): lax.psum(lax.psum((square_one, square_two, square_kv), axis_name='mp'), '...  41.1 us
    unnamed x16, starting transfers between devices  40.2 us
    psum x1, blocking collectives, local(): loss_total = lax.psum(local_loss, ('dp', 'mp'))  37.2 us
    while x260, local copies, waits for them, and re-layouts  17.9 us
    another operation x1, loops' own time, local(): lax.map(one_image, (clean, noise, lowres, aug_noise, timesteps, aug_level...  17.2 us
    all_gather x1, waiting for transfers between devices, local(): piece = lax.all_gather(kv_weight, 'mp', axis=0, tiled=True)  14.8 us
  transfers between devices with their start and end apart: 19, of which 3 were waited for; matrix products, arithmetic and copies ran while one was open for 20% of the time, Pallas kernels for 0%

profile of v1, /device:TPU:0, one launch (start us, length us, event | category | flops | bytes accessed | tf_op | source)
XLA Modules:
  0.0 459.7 jit_solution(2932644069435206900)
XLA Ops:
  8.1 14.8 %all-gather.2.cloned.1.call-done = bf16[4096,256]{1,0:T(8,128)(2,1)} async-done(((bf16[2048,256]{1,0:T(8,128)(2,1)}), bf16[4096,256]{1,0:T(8,128)(2,1)}) %all-gather.2.cloned.1.call-update) | async-done | bytes 2097168 | tf_op jit(solution)/shard_map/all_gather | solution.py:142
  25.9 184.9 %while.19 = (s32[]{:T(128)}, bf16[2,1152,128]{2,1,0:T(8,128)(2,1)}, bf16[2,1152,128]{2,1,0:T(8,128)(2,1)}, bf16[2,128,256]{1,2,0:T(8,128)(2,1)}, f32[2]{0:T(128)...) while((s32[]{:T(128)}, bf16[2,1152,128]{2,1,0:T(8,128)(2,1)}, ...), condition=%wide.region_22.23_spmd, body=%wide.region_0.22_spmd.sunk | while | flops 8245876736 | bytes 325935616 | solution.py:176
  33.1 3.5 fusion.464
  48.2 3.1 fusion.476
  66.6 3.9 multiply_reduce_fusion.17
  88.4 5.1 %select_reduce_fusion.10 = (f32[128]{0:T(128)S(1)}, f32[64,8,9,128]{3,1,2,0:T(8,128)S(1)}) fusion(f32[64,8,9,128]{3,1,2,0:T(8,128)S(1)} %copy-done.8, f32[128]{0:T(128)S(1)} %copy-done.40, pred[8,9]{0,1:T(8,128)(4,1)} %get-tuple-element.841, f32[128]{0:T(128)S(1)} %copy-done.48, f32[128]{0:T(128)S(1)} %copy-done.46, f32[128]{0:T(128)S(1)} %copy-done.50, ...), kind=kOutput, calls=%fused_computation.51.clone.1 | convolution fusion | flops 1360920448 | bytes 6425160 | tf_op jit(solution)/shard_map/while/body/eval_jaxpr/transpose(jvp())/conv_general_dilated | solution.py:63
  98.5 5.0 %fusion.499 = bf16[3,3,128,128,1]{3,2,1,4,0:T(8,128)(2,1)S(1)} fusion(bf16[64,8,9,128,1]{3,1,4,2,0:T(8,128)(2,1)S(1)} %fusion.495, bf16[64,8,9,128,1]{3,1,4,2,0:T(8,128)(2,1)S(1)} %copy.137, bf16[64,8,9,128,1]{3,1,4,2,0:T(8,128)(2,1)S(1)} %fusion.496, f32[128]{0:T(128)S(1)} %fusion.498, pred[8,9]{0,1:T(8,128)(4,1)} %get-tuple-element.841, ...), kind=kOutput, calls=%fused_computation.101.clone.1 | convolution fusion | flops 1360281600 | bytes 8554568 | tf_op jit(solution)/shard_map/while/body/eval_jaxpr/transpose(jvp())/conv_general_dilated | solution.py:63
  106.5 4.8 %fusion.492 = bf16[3,3,128,128,1]{3,2,1,4,0:T(8,128)(2,1)S(1)} fusion(bf16[64,8,9,128,1]{3,0,2,1,4:T(8,128)(2,1)S(1)} %bitcast.331, bf16[64,8,9,128,1]{3,1,2,0,4:T(8,128)(2,1)S(1)} %maximum_bitcast_fusion.8, bf16[64,8,9,128,1]{3,1,2,0,4:T(8,128)(2,1)S(1)} %fusion.491, bf16[64,8,9,128,1]{3,1,2,0,4:T(8,128)(2,1)S(1)} %maximum_bitcast_fusion.9), kind=kOutput, calls=%fused_computation.100.clone.1 | convolution fusion | flops 1348337664 | bytes 5013504 | tf_op jit(solution)/shard_map/while/body/eval_jaxpr/transpose(jvp())/conv_general_dilated | solution.py:63
  123.4 3.5 fusion.464
  130.5 3.0 select_reduce_fusion.8
  138.8 3.1 fusion.476
  157.2 3.9 multiply_reduce_fusion.17
  178.9 4.9 %select_reduce_fusion.10 = (f32[128]{0:T(128)S(1)}, f32[64,8,9,128]{3,1,2,0:T(8,128)S(1)}) fusion(f32[64,8,9,128]{3,1,2,0:T(8,128)S(1)} %copy-done.8, f32[128]{0:T(128)S(1)} %copy-done.40, pred[8,9]{0,1:T(8,128)(4,1)} %get-tuple-element.841, f32[128]{0:T(128)S(1)} %copy-done.48, f32[128]{0:T(128)S(1)} %copy-done.46, f32[128]{0:T(128)S(1)} %copy-done.50, ...), kind=kOutput, calls=%fused_computation.51.clone.1 | convolution fusion | flops 1360920448 | bytes 6425160 | tf_op jit(solution)/shard_map/while/body/eval_jaxpr/transpose(jvp())/conv_general_dilated | solution.py:63
  188.8 5.0 %fusion.499 = bf16[3,3,128,128,1]{3,2,1,4,0:T(8,128)(2,1)S(1)} fusion(bf16[64,8,9,128,1]{3,1,4,2,0:T(8,128)(2,1)S(1)} %fusion.495, bf16[64,8,9,128,1]{3,1,4,2,0:T(8,128)(2,1)S(1)} %copy.137, bf16[64,8,9,128,1]{3,1,4,2,0:T(8,128)(2,1)S(1)} %fusion.496, f32[128]{0:T(128)S(1)} %fusion.498, pred[8,9]{0,1:T(8,128)(4,1)} %get-tuple-element.841, ...), kind=kOutput, calls=%fused_computation.101.clone.1 | convolution fusion | flops 1360281600 | bytes 8554568 | tf_op jit(solution)/shard_map/while/body/eval_jaxpr/transpose(jvp())/conv_general_dilated | solution.py:63
  196.8 5.0 %fusion.492 = bf16[3,3,128,128,1]{3,2,1,4,0:T(8,128)(2,1)S(1)} fusion(bf16[64,8,9,128,1]{3,0,2,1,4:T(8,128)(2,1)S(1)} %bitcast.331, bf16[64,8,9,128,1]{3,1,2,0,4:T(8,128)(2,1)S(1)} %maximum_bitcast_fusion.8, bf16[64,8,9,128,1]{3,1,2,0,4:T(8,128)(2,1)S(1)} %fusion.491, bf16[64,8,9,128,1]{3,1,2,0,4:T(8,128)(2,1)S(1)} %maximum_bitcast_fusion.9), kind=kOutput, calls=%fused_computation.100.clone.1 | convolution fusion | flops 1348337664 | bytes 5013504 | tf_op jit(solution)/shard_map/while/body/eval_jaxpr/transpose(jvp())/conv_general_dilated | solution.py:63
  210.8 3.6 convolution_bitcast_fusion.11
  214.5 13.2 %reduce-scatter.7.cloned.1.call-done = f32[2048,256]{0,1:T(8,128)} async-done(((f32[4096,256]{0,1:T(8,128)}), f32[2048,256]{0,1:T(8,128)}) %reduce-scatter.7.cloned.1.call-update) | async-done | bytes 2097168 | tf_op jit(solution)/shard_map/reduce_scatter | solution.py:193
  229.3 87.8 %fusion.288 = (f32[48,128]{1,0:T(8,128)S(1)}, f32[48,128]{1,0:T(8,128)S(1)}) fusion(f32[1152,128]{1,0:T(8,128)S(1)} %get-tuple-element.472, f32[1152,128]{1,0:T(8,128)S(1)} %get-tuple-element.471), kind=kCustom, calls=%all-reduce-scatter.2 | all-reduce-scatter fusion | flops 393217 | bytes 1228800
  323.6 7.0 %collective-permute-start.7 = (f32[36,128]{1,0:T(8,128)S(1)}, f32[36,128]{1,0:T(8,128)S(1)}, u32[]{:S(2)}, u32[]{:S(2)}) collective-permute-start(f32[36,128]{1,0:T(8,128)S(1)} %slice.90), channel_id=1, source_target_pairs={{0,8},{1,9},{2,10},{3,11},{4,12},{5,13},{6,14},{7,15},{8,16},{9,17... | collective-permute-start | bytes 55304
  333.4 4.9 %collective-permute-start.8 = (f32[48,128]{1,0:T(8,128)S(1)}, f32[48,128]{1,0:T(8,128)S(1)}, u32[]{:S(2)}, u32[]{:S(2)}) collective-permute-start(f32[48,128]{1,0:T(8,128)S(1)} %get-tuple-element.420), channel_id=1, source_target_pairs={{0,1},{1,2},{2,3},{3,4},{4,5},{5,6},{6,7},{7,8},{8,9},{9,10},{10,1... | collective-permute-start | bytes 73736
  343.7 3.2 collective-permute-start.1
  359.6 37.2 %psum.55 = f32[]{:T(128)} all-reduce(f32[]{:T(128)} %reduce_sum.338), channel_id=1, replica_groups=mesh['dp'=16,'mp'=2] {'dp','mp'}, use_global_device_ids=true, to_apply=%region_39.40 | all-reduce | flops 1 | bytes 8 | tf_op jit(solution)/shard_map/psum | solution.py:182
  402.7 3.1 all-reduce.11
  405.8 41.1 %all-reduce.10 = (f32[]{:T(128)}, f32[]{:T(128)}, f32[]{:T(128)}) all-reduce(f32[]{:T(128)} %get-tuple-element.414, f32[]{:T(128)} %get-tuple-element.415, f32[]{:T(128)} %get-tuple-element.416), channel_id=1, replica_groups=mesh['dp'=16,'mp'=2] {'dp'}, use_global_device_ids=true, to_apply=%region_27.28 | all-reduce | flops 3 | bytes 24 | tf_op jit(solution)/shard_map/psum | solution.py:198
  (516 shorter events, 154.6 us)
Async XLA Ops:
  7.2 15.7 %all-gather.2.cloned.1.call-start = ((), (), s32[]{:S(2)}) async-start(), calls=%async_computation.2 | async-start | bytes 3145728 | tf_op jit(solution)/shard_map/all_gather | solution.py:142
  7.9 219.8 %reduce-scatter.7.cloned.1.call-start = ((), (), s32[]{:S(2)}) async-start(), calls=%async_computation.3 | async-start | bytes 6291456 | tf_op jit(solution)/shard_map/reduce_scatter | solution.py:193
  8.0 17.8 %copy-start.26 = (bf16[128,128]{1,0:T(8,128)(2,1)S(1)}, bf16[128,128]{1,0:T(8,128)(2,1)}, u32[]{:S(2)}) copy-start(bf16[128,128]{1,0:T(8,128)(2,1)} %param.31) | copy-start | bytes 98308
  8.0 17.8 %copy-start.30 = (pred[8,9]{0,1:T(8,128)(4,1)S(1)}, pred[8,9]{0,1:T(8,128)(4,1)}, u32[]{:S(2)}) copy-start(pred[8,9]{0,1:T(8,128)(4,1)} %constant.595) | copy-start | bytes 220
  36.6 18.0 %copy-start.67 = (s32[128]{0:T(128)}, s32[128]{0:T(128)S(1)}, u32[]{:S(2)}) copy-start(s32[128]{0:T(128)S(1)} %and_select_fusion.2) | copy-start | bytes 1540 | tf_op jit(solution)/shard_map/while
  126.9 18.2 %copy-start.67 = (s32[128]{0:T(128)}, s32[128]{0:T(128)S(1)}, u32[]{:S(2)}) copy-start(s32[128]{0:T(128)S(1)} %and_select_fusion.2) | copy-start | bytes 1540 | tf_op jit(solution)/shard_map/while
  214.4 186.1 %reduce-scatter.9.cloned.1.call-start = ((), (), s32[]{:S(2)}) async-start(), calls=%async_computation.4 | async-start | bytes 2228224 | tf_op jit(solution)/shard_map/reduce_scatter | solution.py:194
  227.7 131.3 %copy-start.66 = (f32[2]{0:T(128)S(1)}, f32[2]{0:T(128)}, u32[]{:S(2)}) copy-start(f32[2]{0:T(128)} %get-tuple-element.973) | copy-start | bytes 28
  317.1 6.5 %collective-permute-start.15 = (f32[36,128]{1,0:T(8,128)S(1)}, f32[36,128]{1,0:T(8,128)S(1)}, u32[]{:S(2)}, u32[]{:S(2)}) collective-permute-start(f32[36,128]{1,0:T(8,128)S(1)} %slice.91), channel_id=1, source_target_pairs={{0,8},{1,9},{2,10},{3,11},{4,12},{5,13},{6,14},{7,15},{8,16},{9,17... | collective-permute-start | bytes 55304
  318.4 15.0 %collective-permute-start.10 = (f32[48,128]{1,0:T(8,128)S(1)}, f32[48,128]{1,0:T(8,128)S(1)}, u32[]{:S(2)}, u32[]{:S(2)}) collective-permute-start(f32[48,128]{1,0:T(8,128)S(1)} %get-tuple-element.420), channel_id=1, source_target_pairs={{0,3},{1,4},{2,5},{3,6},{4,7},{5,8},{6,9},{7,10},{8,11},{9,12},{10... | collective-permute-start | bytes 73736
  319.7 18.7 %collective-permute-start.11 = (f32[48,128]{1,0:T(8,128)S(1)}, f32[48,128]{1,0:T(8,128)S(1)}, u32[]{:S(2)}, u32[]{:S(2)}) collective-permute-start(f32[48,128]{1,0:T(8,128)S(1)} %get-tuple-element.420), channel_id=1, source_target_pairs={{0,4},{1,5},{2,6},{3,7},{4,8},{5,9},{6,10},{7,11},{8,12},{9,13},{1... | collective-permute-start | bytes 73736
  321.0 20.1 %collective-permute-start.12 = (f32[48,128]{1,0:T(8,128)S(1)}, f32[48,128]{1,0:T(8,128)S(1)}, u32[]{:S(2)}, u32[]{:S(2)}) collective-permute-start(f32[48,128]{1,0:T(8,128)S(1)} %get-tuple-element.420), channel_id=1, source_target_pairs={{0,5},{1,6},{2,7},{3,8},{4,9},{5,10},{6,11},{7,12},{8,13},{9,14},{... | collective-permute-start | bytes 73736
  322.3 21.4 %collective-permute-start.13 = (f32[48,128]{1,0:T(8,128)S(1)}, f32[48,128]{1,0:T(8,128)S(1)}, u32[]{:S(2)}, u32[]{:S(2)}) collective-permute-start(f32[48,128]{1,0:T(8,128)S(1)} %get-tuple-element.420), channel_id=1, source_target_pairs={{0,6},{1,7},{2,8},{3,9},{4,10},{5,11},{6,12},{7,13},{8,14},{9,15},... | collective-permute-start | bytes 73736
  323.6 8.5 %collective-permute-start.7 = (f32[36,128]{1,0:T(8,128)S(1)}, f32[36,128]{1,0:T(8,128)S(1)}, u32[]{:S(2)}, u32[]{:S(2)}) collective-permute-start(f32[36,128]{1,0:T(8,128)S(1)} %slice.90), channel_id=1, source_target_pairs={{0,8},{1,9},{2,10},{3,11},{4,12},{5,13},{6,14},{7,15},{8,16},{9,17... | collective-permute-start | bytes 55304
  332.1 14.8 %collective-permute-start.14 = (f32[48,128]{1,0:T(8,128)S(1)}, f32[48,128]{1,0:T(8,128)S(1)}, u32[]{:S(2)}, u32[]{:S(2)}) collective-permute-start(f32[48,128]{1,0:T(8,128)S(1)} %get-tuple-element.420), channel_id=1, source_target_pairs={{0,7},{1,8},{2,9},{3,10},{4,11},{5,12},{6,13},{7,14},{8,15},{9,16}... | collective-permute-start | bytes 73736
  333.4 16.5 %collective-permute-start.8 = (f32[48,128]{1,0:T(8,128)S(1)}, f32[48,128]{1,0:T(8,128)S(1)}, u32[]{:S(2)}, u32[]{:S(2)}) collective-permute-start(f32[48,128]{1,0:T(8,128)S(1)} %get-tuple-element.420), channel_id=1, source_target_pairs={{0,1},{1,2},{2,3},{3,4},{4,5},{5,6},{6,7},{7,8},{8,9},{9,10},{10,1... | collective-permute-start | bytes 73736
  338.4 14.0 %collective-permute-start.9 = (f32[48,128]{1,0:T(8,128)S(1)}, f32[48,128]{1,0:T(8,128)S(1)}, u32[]{:S(2)}, u32[]{:S(2)}) collective-permute-start(f32[48,128]{1,0:T(8,128)S(1)} %get-tuple-element.420), channel_id=1, source_target_pairs={{0,2},{1,3},{2,4},{3,5},{4,6},{5,7},{6,8},{7,9},{8,10},{9,11},{10,... | collective-permute-start | bytes 73736
  341.1 13.2 %collective-permute-start = (f32[48,128]{1,0:T(8,128)S(1)}, f32[48,128]{1,0:T(8,128)S(1)}, u32[]{:S(2)}, u32[]{:S(2)}) collective-permute-start(f32[48,128]{1,0:T(8,128)S(1)} %get-tuple-element.419), channel_id=1, source_target_pairs={{0,1},{1,2},{2,3},{3,4},{4,5},{5,6},{6,7},{7,8},{8,9},{9,10},{10,1... | collective-permute-start | bytes 73736
  343.7 13.6 %collective-permute-start.1 = (f32[48,128]{1,0:T(8,128)S(1)}, f32[48,128]{1,0:T(8,128)S(1)}, u32[]{:S(2)}, u32[]{:S(2)}) collective-permute-start(f32[48,128]{1,0:T(8,128)S(1)} %get-tuple-element.419), channel_id=1, source_target_pairs={{0,2},{1,3},{2,4},{3,5},{4,6},{5,7},{6,8},{7,9},{8,10},{9,11},{10,... | collective-permute-start | bytes 73736
  347.0 51.0 %collective-permute-start.2 = (f32[48,128]{1,0:T(8,128)S(1)}, f32[48,128]{1,0:T(8,128)S(1)}, u32[]{:S(2)}, u32[]{:S(2)}) collective-permute-start(f32[48,128]{1,0:T(8,128)S(1)} %get-tuple-element.419), channel_id=1, source_target_pairs={{0,3},{1,4},{2,5},{3,6},{4,7},{5,8},{6,9},{7,10},{8,11},{9,12},{10... | collective-permute-start | bytes 73736
  349.9 48.1 %collective-permute-start.3 = (f32[48,128]{1,0:T(8,128)S(1)}, f32[48,128]{1,0:T(8,128)S(1)}, u32[]{:S(2)}, u32[]{:S(2)}) collective-permute-start(f32[48,128]{1,0:T(8,128)S(1)} %get-tuple-element.419), channel_id=1, source_target_pairs={{0,4},{1,5},{2,6},{3,7},{4,8},{5,9},{6,10},{7,11},{8,12},{9,13},{1... | collective-permute-start | bytes 73736
  352.3 45.7 %collective-permute-start.4 = (f32[48,128]{1,0:T(8,128)S(1)}, f32[48,128]{1,0:T(8,128)S(1)}, u32[]{:S(2)}, u32[]{:S(2)}) collective-permute-start(f32[48,128]{1,0:T(8,128)S(1)} %get-tuple-element.419), channel_id=1, source_target_pairs={{0,5},{1,6},{2,7},{3,8},{4,9},{5,10},{6,11},{7,12},{8,13},{9,14},{... | collective-permute-start | bytes 73736
  354.4 43.7 %collective-permute-start.5 = (f32[48,128]{1,0:T(8,128)S(1)}, f32[48,128]{1,0:T(8,128)S(1)}, u32[]{:S(2)}, u32[]{:S(2)}) collective-permute-start(f32[48,128]{1,0:T(8,128)S(1)} %get-tuple-element.419), channel_id=1, source_target_pairs={{0,6},{1,7},{2,8},{3,9},{4,10},{5,11},{6,12},{7,13},{8,14},{9,15},... | collective-permute-start | bytes 73736
  357.4 40.7 %collective-permute-start.6 = (f32[48,128]{1,0:T(8,128)S(1)}, f32[48,128]{1,0:T(8,128)S(1)}, u32[]{:S(2)}, u32[]{:S(2)}) collective-permute-start(f32[48,128]{1,0:T(8,128)S(1)} %get-tuple-element.419), channel_id=1, source_target_pairs={{0,7},{1,8},{2,9},{3,10},{4,11},{5,12},{6,13},{7,14},{8,15},{9,16}... | collective-permute-start | bytes 73736
  (129 other events, 388.8 us)
Sparse Core Ops, SparseCore 0:
  9.5 13.2 all-gather.1
  214.5 13.0 reduce-scatter.6
  230.0 82.6 reduce-scatter.8
